TPU v7x, 32 devices: a whole 2x2x4 slice. The times are simulated.
32 devices in a mesh: patch: 16 (over z, y, x), pix: 2 (over core).
Axes of the slice: x: 2, y: 2, z: 4, core: 2. Of those that a mesh axis runs over, the one named last changes fastest.
Arguments:
- pixel_pos: float32 [2, 3072], P(None, ('patch', 'pix')), may hold values from -4 to 4
- pixel_view: float32 [3, 3072], P(None, ('patch', 'pix')), may hold values from -1 to 1
- observed: float32 [3072], P(('patch', 'pix')), may hold values from -6 to 6
- noise_scale: float32 [3072], P(('patch', 'pix')), may hold values from 0.5 to 2
- valid_mask: int32 [3072], P(('patch', 'pix')), may hold values 0 or 1
- patch_pos: float32 [2, 768], P(None, 'patch'), may hold values from -4 to 4
- patch_depth: float32 [768], P('patch'), may hold values from 0.3 to 1.5
- segment_ids: int32 [768], P('patch'), may hold values from 0 to 15, never falling along the last dimension, each value on 1 to 192 neighbouring positions
- seg_strike: float32 [16], replicated, may hold values from -3.140625 to 3.140625
- seg_dip: float32 [16], replicated, may hold values from 0.35 to 1.4
- slip_models: bfloat16 [768, 3, 128], P('patch'), may hold values from -0.8984375 to 0.8984375
Outputs:
- residual: float32 [3072, 128], P(('patch', 'pix'))
- misfit: float32 [128], replicated
Inputs may be any that keep to these rules, and one draw needn't show every extreme that they name: `segment_ids`: segment ids never fall along the patches.
All inputs are finite; a program needn't handle non-finite values. No bound on the sum of `valid_mask` on one device may be relied on, other than what follows from the above.
Results may differ from a plain program's by a relative error of at most 0.0003.
Values may be sent and summed in bfloat16 or wider, within the bound.
A program may use at most 64 MiB of HBM per device.

v0:
```python
import math
import jax
import jax.numpy as jnp
from jax import lax
from jax.sharding import PartitionSpec as P

two_pi = 2.0 * math.pi
mu_ratio = 0.5


def partner(value, axis, distance):
    mask = 2**distance
    pairs = [(source, source ^ mask) for source in range(lax.axis_size(axis))]
    return lax.ppermute(value, axis, pairs)


def point_green(pixel_pos, pixel_view, frame_rows):
    src_east = frame_rows[0][:, None]
    src_north = frame_rows[1][:, None]
    src_depth = frame_rows[2][:, None]
    sin_strike = frame_rows[3][:, None]
    cos_strike = frame_rows[4][:, None]
    sin_dip = frame_rows[5][:, None]
    cos_dip = frame_rows[6][:, None]
    east_gap = pixel_pos[0][None, :] - src_east
    north_gap = pixel_pos[1][None, :] - src_north
    along_x = east_gap * sin_strike + north_gap * cos_strike
    across = north_gap * sin_strike - east_gap * cos_strike
    depth_term = across * cos_dip + src_depth * sin_dip
    plane_term = across * sin_dip - src_depth * cos_dip
    radius = jnp.sqrt(along_x * along_x + across * across + src_depth * src_depth)
    over_r = 1.0 / radius
    over_r3 = over_r * over_r * over_r
    over_r5 = over_r3 * over_r * over_r
    over_rd = 1.0 / (radius + src_depth)
    base_term = over_r * over_rd * over_rd
    cubic_term = (3.0 * radius + src_depth) * over_r3 * over_rd * over_rd * over_rd
    square_term = (2.0 * radius + src_depth) * over_r3 * over_rd * over_rd
    term_one = mu_ratio * across * (base_term - along_x * along_x * cubic_term)
    term_two = mu_ratio * along_x * (base_term - across * across * cubic_term)
    term_three = mu_ratio * along_x * over_r3 - term_two
    term_four = -mu_ratio * along_x * across * square_term
    term_five = mu_ratio * (over_r * over_rd - along_x * along_x * square_term)
    scaled_q = 3.0 * plane_term * over_r5
    dip_mixed = sin_dip * cos_dip
    dip_square = sin_dip * sin_dip
    strike_x = -(scaled_q * along_x * along_x + term_one * sin_dip)
    strike_y = -(scaled_q * along_x * across + term_two * sin_dip)
    strike_z = -(scaled_q * along_x * src_depth + term_four * sin_dip)
    dip_x = -(scaled_q * along_x * depth_term - term_three * dip_mixed)
    dip_y = -(scaled_q * across * depth_term - term_one * dip_mixed)
    dip_z = -(scaled_q * src_depth * depth_term - term_five * dip_mixed)
    open_x = scaled_q * along_x * plane_term - term_three * dip_square
    open_y = scaled_q * across * plane_term - term_one * dip_square
    open_z = scaled_q * src_depth * plane_term - term_five * dip_square

    def project(comp_x, comp_y, comp_z):
        east_move = comp_x * sin_strike - comp_y * cos_strike
        north_move = comp_x * cos_strike + comp_y * sin_strike
        return (
            pixel_view[0][None, :] * east_move
            + pixel_view[1][None, :] * north_move
            + pixel_view[2][None, :] * comp_z
        ) / two_pi

    return jnp.stack(
        [
            project(strike_x, strike_y, strike_z),
            project(dip_x, dip_y, dip_z),
            project(open_x, open_y, open_z),
        ],
        axis=1,
    )


def local_frames(patch_pos, patch_depth, segment_ids, seg_strike, seg_dip):
    segment_count = seg_strike.shape[0]
    matches = segment_ids[:, None] == jnp.arange(segment_count, dtype=jnp.int32)[None, :]
    strike = jnp.sum(jnp.where(matches, seg_strike[None, :], 0.0), axis=1)
    dip_angle = jnp.sum(jnp.where(matches, seg_dip[None, :], 0.0), axis=1)
    return jnp.stack(
        [
            patch_pos[0],
            patch_pos[1],
            patch_depth,
            jnp.sin(strike),
            jnp.cos(strike),
            jnp.sin(dip_angle),
            jnp.cos(dip_angle),
        ],
        axis=0,
    )


def tile_product(site_pos, site_view, frame_rows, slip_table):
    pixel_count = site_pos.shape[1]
    green_tile = point_green(site_pos, site_view, frame_rows).astype(jnp.bfloat16)
    green_tile = green_tile.reshape(frame_rows.shape[1] * 3, pixel_count)
    return lax.dot_general(
        green_tile, slip_table, (((0,), (0,)), ((), ())), preferred_element_type=jnp.float32
    )


def patch_blocks(pixel_pos, pixel_view, frame_rows, slip_piece, running):
    patch_count = slip_piece.shape[0]
    samples = slip_piece.shape[2]
    block_len = min(patch_count, 640)
    full_blocks = patch_count // block_len
    remainder = patch_count - full_blocks * block_len
    head = full_blocks * block_len
    head_frames = frame_rows[:, :head].reshape(7, full_blocks, block_len).transpose(1, 0, 2)
    head_slip = slip_piece[:head].reshape(full_blocks, block_len * 3, samples)

    def add_tile(accum, block_items):
        return (accum + tile_product(pixel_pos, pixel_view, block_items[0], block_items[1]), None)

    running, _ = lax.scan(add_tile, running, (head_frames, head_slip))
    if remainder > 0:
        tail_slip = slip_piece[head:].reshape(remainder * 3, samples)
        running = running + tile_product(pixel_pos, pixel_view, frame_rows[:, head:], tail_slip)
    return running


def index_bit(level):
    return lax.axis_index("patch") // 2**level % 2 == 1


def join_pair(mine, other, upper, axis_dim):
    first = jnp.where(upper, other, mine)
    second = jnp.where(upper, mine, other)
    return jnp.concatenate([first, second], axis=axis_dim)


def per_device(
    pixel_pos,
    pixel_view,
    observed,
    noise_scale,
    valid_mask,
    patch_pos,
    patch_depth,
    segment_ids,
    seg_strike,
    seg_dip,
    slip_models,
):
    own_pixels = pixel_pos.shape[1]
    samples = slip_models.shape[2]
    frames = local_frames(patch_pos, patch_depth, segment_ids, seg_strike, seg_dip)
    total_bits = lax.axis_size("patch").bit_length() - 1
    low_count = (total_bits + 1) // 2
    group_slip = slip_models
    group_frames = frames
    for level in range(low_count):
        upper = index_bit(level)
        other_slip = partner(group_slip, "patch", level)
        other_frames = partner(group_frames, "patch", level)
        group_slip = join_pair(group_slip, other_slip, upper, 0)
        group_frames = join_pair(group_frames, other_frames, upper, 1)
    group_sites = jnp.concatenate([pixel_pos, pixel_view], axis=0)
    for level in range(low_count, total_bits):
        upper = index_bit(level)
        other_sites = partner(group_sites, "patch", level)
        group_sites = join_pair(group_sites, other_sites, upper, 1)
    site_groups = group_sites.shape[1] // own_pixels
    stacked = group_sites.reshape(5, site_groups, own_pixels).transpose(1, 0, 2)

    def one_group(block_sites):
        start = jnp.zeros((own_pixels, samples), jnp.float32)
        return patch_blocks(block_sites[:2], block_sites[2:], group_frames, group_slip, start)

    partial_value = lax.map(one_group, stacked).reshape(site_groups * own_pixels, samples)
    for level in range(total_bits - 1, low_count - 1, -1):
        upper = index_bit(level)
        half = partial_value.shape[0] // 2
        keep = jnp.where(upper, partial_value[half:], partial_value[:half])
        send = jnp.where(upper, partial_value[:half], partial_value[half:])
        partial_value = keep + partner(send, "patch", level)
    residual = (
        valid_mask.astype(jnp.float32)[:, None]
        * (partial_value - observed[:, None])
        / noise_scale[:, None]
    )
    own_sum = jnp.sum(residual * residual, axis=0)
    pixels = own_pixels * lax.axis_size("patch") * lax.axis_size("pix")
    misfit = lax.psum(own_sum, ("patch", "pix")) / pixels
    return (residual, misfit)


def solution(mesh):
    return jax.shard_map(
        per_device,
        mesh=mesh,
        in_specs=(
            P(None, ("patch", "pix")),
            P(None, ("patch", "pix")),
            P(("patch", "pix")),
            P(("patch", "pix")),
            P(("patch", "pix")),
            P(None, "patch"),
            P("patch"),
            P("patch"),
            P(),
            P(),
            P("patch", None, None),
        ),
        out_specs=(P(("patch", "pix"), None), P()),
        check_vma=False,
    )
```

profile of v0, /device:TPU:0, one launch (start us, length us, event | category | flops | bytes accessed | tf_op | source)
XLA Modules:
  0.0 74.1 jit_solution(12593632684655895281)
XLA Ops:
  0.6 3.0 %collective-permute-start.4 = (bf16[48,3,128]{2,0,1:T(8,128)(2,1)}, bf16[48,3,128]{2,0,1:T(8,128)(2,1)S(1)}, u32[]{:S(2)}, u32[]{:S(2)}) collective-permute-start(bf16[48,3,128]{2,0,1:T(8,128)(2,1)} %param.23), channel_id=1, source_target_pairs={{0,2},{2,0},{4,6},{6,4},{8,10},{10,8},{12,14},{14,12},{16,18},{18,... | collective-permute-start | bytes 110600 | tf_op jit(solution)/shard_map/ppermute | solution.py:14
  3.7 0.8 %select_reduce_fusion = (f32[48]{0:T(128)S(1)}, f32[48]{0:T(128)S(1)}) fusion(f32[16]{0:T(128)} %param.22, s32[48]{0:T(128)} %param.20, f32[16]{0:T(128)} %param.21), kind=kLoop, calls=%fused_computation.120 | loop fusion | flops 3744 | bytes 704 | tf_op jit(solution)/shard_map/reduce_sum | solution.py:80
  4.5 0.7 copy-done.3
  5.2 0.1 collective-permute-start.2
  5.3 0.6 copy-done.1
  5.9 1.6 %collective-permute-start = (f32[5,96]{1,0:T(8,128)S(1)}, f32[5,96]{1,0:T(8,128)S(1)}, u32[]{:S(2)}, u32[]{:S(2)}) collective-permute-start(f32[5,96]{1,0:T(8,128)S(1)} %pad_maximum_fusion.5), channel_id=1, source_target_pairs={{0,8},{2,10},{4,12},{6,14},{8,0},{10,2},{12,4},{14,6},{16,24},{18,... | collective-permute-start | bytes 5768 | tf_op jit(solution)/shard_map/ppermute | solution.py:14
  7.5 1.4 %collective-permute-done.2 = f32[7,48]{1,0:T(8,128)S(1)} collective-permute-done((f32[7,48]{1,0:T(8,128)S(1)}, f32[7,48]{1,0:T(8,128)S(1)}, u32[]{:S(2)}, u32[]{:S(2)}) %collective-permute-start.2) | collective-permute-done | bytes 1376 | tf_op jit(solution)/shard_map/ppermute | solution.py:14
  8.9 0.1 pad_maximum_fusion.6
  9.0 1.5 %collective-permute-start.3 = (f32[7,96]{1,0:T(8,128)S(1)}, f32[7,96]{1,0:T(8,128)S(1)}, u32[]{:S(2)}, u32[]{:S(2)}) collective-permute-start(f32[7,96]{1,0:T(8,128)S(1)} %pad_maximum_fusion.6), channel_id=1, source_target_pairs={{0,4},{2,6},{4,0},{6,2},{8,12},{10,14},{12,8},{14,10},{16,20},{18,... | collective-permute-start | bytes 8072 | tf_op jit(solution)/shard_map/ppermute | solution.py:14
  10.6 2.6 %collective-permute-start.1 = (f32[5,192]{1,0:T(8,128)S(1)}, f32[5,192]{1,0:T(8,128)S(1)}, u32[]{:S(2)}, u32[]{:S(2)}) collective-permute-start(f32[5,192]{1,0:T(8,128)S(1)} %pad_maximum_fusion.4), channel_id=1, source_target_pairs={{0,16},{2,18},{4,20},{6,22},{8,24},{10,26},{12,28},{14,30},{16,0},... | collective-permute-start | bytes 11528 | tf_op jit(solution)/shard_map/ppermute | solution.py:14
  13.2 0.1 multiply_bitcast_fusion
  13.3 0.1 multiply_bitcast_fusion.1
  13.5 1.6 %collective-permute-done.1 = f32[5,192]{1,0:T(8,128)S(1)} collective-permute-done((f32[5,192]{1,0:T(8,128)S(1)}, f32[5,192]{1,0:T(8,128)S(1)}, u32[]{:S(2)}, u32[]{:S(2)}) %collective-permute-start.1) | collective-permute-done | bytes 3872 | tf_op jit(solution)/shard_map/ppermute | solution.py:14
  15.2 0.7 collective-permute-start.5
  16.0 0.1 reshape.2726
  16.0 3.6 %collective-permute-done.5 = bf16[96,3,128]{2,0,1:T(8,128)(2,1)S(1)} collective-permute-done((bf16[96,3,128]{2,0,1:T(8,128)(2,1)S(1)}, bf16[96,3,128]{2,0,1:T(8,128)(2,1)S(1)}, u32[]{:S(2)}, u32[]{:S(2)}) %collective-permute-start.5) | collective-permute-done | bytes 73760 | tf_op jit(solution)/shard_map/ppermute | solution.py:14
  19.7 3.4 %while.11 = (s32[]{:T(128)}, f32[4,96,128]{2,1,0:T(8,128)S(1)}, f32[4,5,96]{2,0,1:T(4,128)S(1)}, f32[7,192]{1,0:T(8,128)S(1)}, f32[192,1]{0,1:T(1,128)S(1)}, /*i...) while((s32[]{:T(128)}, f32[4,96,128]{2,1,0:T(8,128)S(1)}, ...), condition=%wide.region_3.4_spmd, body=%wide.region_2.3_spmd.sunk | while | flops 16626054 | bytes 485213 | solution.py:172
  19.8 0.5 fusion.98
  20.3 0.2 fusion.99
  20.6 0.5 fusion.98
  21.2 0.2 fusion.99
  21.5 0.5 fusion.98
  22.0 0.2 fusion.99
  22.3 0.5 fusion.98
  22.9 0.2 fusion.99
  23.1 2.7 %collective-permute-start.6 = (f32[192,128]{1,0:T(8,128)S(1)}, f32[192,128]{1,0:T(8,128)S(1)}, u32[]{:S(2)}, u32[]{:S(2)}) collective-permute-start(f32[192,128]{1,0:T(8,128)S(1)} %bitcast.102), channel_id=1, source_target_pairs={{0,16},{2,18},{4,20},{6,22},{8,24},{10,26},{12,28},{14,30},{16,0},... | collective-permute-start | bytes 294920 | tf_op jit(solution)/shard_map/ppermute | solution.py:14
  25.8 2.9 %collective-permute-done.6 = f32[192,128]{1,0:T(8,128)S(1)} collective-permute-done((f32[192,128]{1,0:T(8,128)S(1)}, f32[192,128]{1,0:T(8,128)S(1)}, u32[]{:S(2)}, u32[]{:S(2)}) %collective-permute-start.6) | collective-permute-done | bytes 98336 | tf_op jit(solution)/shard_map/ppermute | solution.py:14
  28.8 2.2 %collective-permute-start.7 = (f32[96,128]{1,0:T(8,128)S(1)}, f32[96,128]{1,0:T(8,128)S(1)}, u32[]{:S(2)}, u32[]{:S(2)}) collective-permute-start(f32[96,128]{1,0:T(8,128)S(1)} %slice_select_fusion.2), channel_id=1, source_target_pairs={{0,8},{2,10},{4,12},{6,14},{8,0},{10,2},{12,4},{14,6},{16,24},{18,... | collective-permute-start | bytes 147464 | tf_op jit(solution)/shard_map/ppermute | solution.py:14
  31.0 2.1 %collective-permute-done.7 = f32[96,128]{1,0:T(8,128)S(1)} collective-permute-done((f32[96,128]{1,0:T(8,128)S(1)}, f32[96,128]{1,0:T(8,128)S(1)}, u32[]{:S(2)}, u32[]{:S(2)}) %collective-permute-start.7) | collective-permute-done | bytes 49184 | tf_op jit(solution)/shard_map/ppermute | solution.py:14
  33.0 0.7 multiply_reduce_fusion
  33.8 39.8 %psum.7 = f32[128]{0:T(128)S(1)} all-reduce(f32[128]{0:T(128)S(1)} %get-tuple-element.127), channel_id=1, replica_groups=mesh['patch'=16,'pix'=2] {'patch','pix'}, use_global_device_ids=true, to_apply=%region_5.6 | all-reduce | flops 128 | bytes 1024 | tf_op jit(solution)/shard_map/psum | solution.py:186
  73.6 0.5 broadcast_multiply_fusion.2
  (49 shorter events, 0.8 us)
Async XLA Ops:
  0.6 14.6 %collective-permute-start.4 = (bf16[48,3,128]{2,0,1:T(8,128)(2,1)}, bf16[48,3,128]{2,0,1:T(8,128)(2,1)S(1)}, u32[]{:S(2)}, u32[]{:S(2)}) collective-permute-start(bf16[48,3,128]{2,0,1:T(8,128)(2,1)} %param.23), channel_id=1, source_target_pairs={{0,2},{2,0},{4,6},{6,4},{8,10},{10,8},{12,14},{14,12},{16,18},{18,... | collective-permute-start | bytes 110600 | tf_op jit(solution)/shard_map/ppermute | solution.py:14
  4.5 0.7 copy-start.3
  4.5 0.7 copy-start.6
  5.2 0.7 copy-start.1
  5.2 0.7 copy-start.2
  5.2 3.7 %collective-permute-start.2 = (f32[7,48]{1,0:T(8,128)S(1)}, f32[7,48]{1,0:T(8,128)S(1)}, u32[]{:S(2)}, u32[]{:S(2)}) collective-permute-start(f32[7,48]{1,0:T(8,128)S(1)} %stack.24), channel_id=1, source_target_pairs={{0,2},{2,0},{4,6},{6,4},{8,10},{10,8},{12,14},{14,12},{16,18},{18,... | collective-permute-start | bytes 4040 | tf_op jit(solution)/shard_map/ppermute | solution.py:14
  5.9 4.6 %collective-permute-start = (f32[5,96]{1,0:T(8,128)S(1)}, f32[5,96]{1,0:T(8,128)S(1)}, u32[]{:S(2)}, u32[]{:S(2)}) collective-permute-start(f32[5,96]{1,0:T(8,128)S(1)} %pad_maximum_fusion.5), channel_id=1, source_target_pairs={{0,8},{2,10},{4,12},{6,14},{8,0},{10,2},{12,4},{14,6},{16,24},{18,... | collective-permute-start | bytes 5768 | tf_op jit(solution)/shard_map/ppermute | solution.py:14
  9.0 4.2 %collective-permute-start.3 = (f32[7,96]{1,0:T(8,128)S(1)}, f32[7,96]{1,0:T(8,128)S(1)}, u32[]{:S(2)}, u32[]{:S(2)}) collective-permute-start(f32[7,96]{1,0:T(8,128)S(1)} %pad_maximum_fusion.6), channel_id=1, source_target_pairs={{0,4},{2,6},{4,0},{6,2},{8,12},{10,14},{12,8},{14,10},{16,20},{18,... | collective-permute-start | bytes 8072 | tf_op jit(solution)/shard_map/ppermute | solution.py:14
  10.6 4.6 %collective-permute-start.1 = (f32[5,192]{1,0:T(8,128)S(1)}, f32[5,192]{1,0:T(8,128)S(1)}, u32[]{:S(2)}, u32[]{:S(2)}) collective-permute-start(f32[5,192]{1,0:T(8,128)S(1)} %pad_maximum_fusion.4), channel_id=1, source_target_pairs={{0,16},{2,18},{4,20},{6,22},{8,24},{10,26},{12,28},{14,30},{16,0},... | collective-permute-start | bytes 11528 | tf_op jit(solution)/shard_map/ppermute | solution.py:14
  13.3 1.9 %copy-start = (bf16[48,3,128]{2,0,1:T(8,128)(2,1)S(1)}, bf16[48,3,128]{2,0,1:T(8,128)(2,1)}, u32[]{:S(2)}) copy-start(bf16[48,3,128]{2,0,1:T(8,128)(2,1)} %param.23) | copy-start | bytes 110596
  15.2 4.4 %collective-permute-start.5 = (bf16[96,3,128]{2,0,1:T(8,128)(2,1)S(1)}, bf16[96,3,128]{2,0,1:T(8,128)(2,1)S(1)}, u32[]{:S(2)}, u32[]{:S(2)}) collective-permute-start(bf16[96,3,128]{2,0,1:T(8,128)(2,1)S(1)} %pad_maximum_fusion.1), channel_id=1, source_target_pairs={{0,4},{2,6},{4,0},{6,2},{8,12},{10,14},{12,8},{14,10},{16,20},{18,... | collective-permute-start | bytes 221192 | tf_op jit(solution)/shard_map/ppermute | solution.py:14
  23.1 5.6 %collective-permute-start.6 = (f32[192,128]{1,0:T(8,128)S(1)}, f32[192,128]{1,0:T(8,128)S(1)}, u32[]{:S(2)}, u32[]{:S(2)}) collective-permute-start(f32[192,128]{1,0:T(8,128)S(1)} %bitcast.102), channel_id=1, source_target_pairs={{0,16},{2,18},{4,20},{6,22},{8,24},{10,26},{12,28},{14,30},{16,0},... | collective-permute-start | bytes 294920 | tf_op jit(solution)/shard_map/ppermute | solution.py:14
  28.7 2.2 %copy-start.7 = (s32[96]{0:T(128)S(1)}, s32[96]{0:T(128)}, u32[]{:S(2)}) copy-start(s32[96]{0:T(128)} %param.17) | copy-start | bytes 1156
  28.8 4.3 %copy-start.4 = (f32[96]{0:T(128)S(1)}, f32[96]{0:T(128)}, u32[]{:S(2)}) copy-start(f32[96]{0:T(128)} %param.16) | copy-start | bytes 1156
  28.8 4.2 %copy-start.5 = (f32[96]{0:T(128)S(1)}, f32[96]{0:T(128)}, u32[]{:S(2)}) copy-start(f32[96]{0:T(128)} %param.15) | copy-start | bytes 1156
  28.8 4.2 %collective-permute-start.7 = (f32[96,128]{1,0:T(8,128)S(1)}, f32[96,128]{1,0:T(8,128)S(1)}, u32[]{:S(2)}, u32[]{:S(2)}) collective-permute-start(f32[96,128]{1,0:T(8,128)S(1)} %slice_select_fusion.2), channel_id=1, source_target_pairs={{0,8},{2,10},{4,12},{6,14},{8,0},{10,2},{12,4},{14,6},{16,24},{18,... | collective-permute-start | bytes 147464 | tf_op jit(solution)/shard_map/ppermute | solution.py:14
where the time goes:
time: 74.4 us; the launch traced here: 74.1 us
  blocking collectives  39.8 us (53%)
  starting transfers between devices  14.3 us (19%)
  waiting for transfers between devices  11.6 us (16%)
  other arithmetic  4.89 us (7%)
  local copies, waits for them, and re-layouts  1.55 us (2%)
  matrix products  0.95 us (1%)
  between operations  0.75 us (1%)
    psum x1, blocking collectives, per_device(): misfit = lax.psum(own_sum, ('patch', 'pix')) / pixels  39.8 us
    ppermute x8, starting transfers between devices, partner(): return lax.ppermute(value, axis, pairs)  14.3 us
    ppermute x8, waiting for transfers between devices, partner(): return lax.ppermute(value, axis, pairs)  11.6 us
    another operation x4, other arithmetic  2.11 us
  transfers between devices with their start and end apart: 8, of which 5 were waited for; matrix products, arithmetic and copies ran while one was open for 2% of the time, Pallas kernels for 0%

commit v1 on v0

--- a/solution.py
+++ b/solution.py
@@ -6,6 +6,11 @@
 
 two_pi = 2.0 * math.pi
 mu_ratio = 0.5
+
+
+def summed_here(block, axis):
+    parts = lax.all_gather(block, axis)
+    return jnp.sum(parts, axis=0)
 
 
 def partner(value, axis, distance):
@@ -183,7 +188,7 @@
     )
     own_sum = jnp.sum(residual * residual, axis=0)
     pixels = own_pixels * lax.axis_size("patch") * lax.axis_size("pix")
-    misfit = lax.psum(own_sum, ("patch", "pix")) / pixels
+    misfit = summed_here(own_sum, ("patch", "pix")) / pixels
     return (residual, misfit)
 
 

time: 74.4 us -> 76.2 us (1.024)
  blocking collectives: 39.8 us -> 41.7 us
    all_gather x0 -> x1, blocking collectives: none -> 41.7 us  [summed_here(): parts = lax.all_gather(block, axis)]
    psum x1 -> x0, blocking collectives: 39.8 us -> none  [per_device(): misfit = lax.psum(own_sum, ('patch', 'pix')) / pixels]
where the time goes in v1:
time: 76.2 us; the launch traced here: 76 us
  blocking collectives  41.7 us (55%)
  starting transfers between devices  14.3 us (19%)
  waiting for transfers between devices  11.6 us (15%)
  other arithmetic  4.94 us (6%)
  local copies, waits for them, and re-layouts  1.55 us (2%)
  matrix products  0.95 us (1%)
    all_gather x1, blocking collectives, summed_here(): parts = lax.all_gather(block, axis)  41.7 us
    ppermute x8, starting transfers between devices, partner(): return lax.ppermute(value, axis, pairs)  14.3 us
    ppermute x8, waiting for transfers between devices, partner(): return lax.ppermute(value, axis, pairs)  11.6 us
    another operation x4, other arithmetic  2.11 us
  transfers between devices with their start and end apart: 8, of which 5 were waited for; matrix products, arithmetic and copies ran while one was open for 2% of the time, Pallas kernels for 0%

profile of v1, /device:TPU:0, one launch (start us, length us, event | category | flops | bytes accessed | tf_op | source)
XLA Modules:
  0.0 76.0 jit_solution(5165784182554445836)
XLA Ops:
  0.6 3.0 %collective-permute-start.4 = (bf16[48,3,128]{2,0,1:T(8,128)(2,1)}, bf16[48,3,128]{2,0,1:T(8,128)(2,1)S(1)}, u32[]{:S(2)}, u32[]{:S(2)}) collective-permute-start(bf16[48,3,128]{2,0,1:T(8,128)(2,1)} %param.23), channel_id=1, source_target_pairs={{0,2},{2,0},{4,6},{6,4},{8,10},{10,8},{12,14},{14,12},{16,18},{18,... | collective-permute-start | bytes 110600 | tf_op jit(solution)/shard_map/ppermute | solution.py:19
  3.7 0.8 %select_reduce_fusion = (f32[48]{0:T(128)S(1)}, f32[48]{0:T(128)S(1)}) fusion(f32[16]{0:T(128)} %param.22, s32[48]{0:T(128)} %param.20, f32[16]{0:T(128)} %param.21), kind=kLoop, calls=%fused_computation.120 | loop fusion | flops 3744 | bytes 704 | tf_op jit(solution)/shard_map/reduce_sum | solution.py:85
  4.5 0.7 copy-done.3
  5.2 0.1 collective-permute-start.2
  5.3 0.6 copy-done.1
  5.9 1.6 %collective-permute-start = (f32[5,96]{1,0:T(8,128)S(1)}, f32[5,96]{1,0:T(8,128)S(1)}, u32[]{:S(2)}, u32[]{:S(2)}) collective-permute-start(f32[5,96]{1,0:T(8,128)S(1)} %pad_maximum_fusion.5), channel_id=1, source_target_pairs={{0,8},{2,10},{4,12},{6,14},{8,0},{10,2},{12,4},{14,6},{16,24},{18,... | collective-permute-start | bytes 5768 | tf_op jit(solution)/shard_map/ppermute | solution.py:19
  7.5 1.4 %collective-permute-done.2 = f32[7,48]{1,0:T(8,128)S(1)} collective-permute-done((f32[7,48]{1,0:T(8,128)S(1)}, f32[7,48]{1,0:T(8,128)S(1)}, u32[]{:S(2)}, u32[]{:S(2)}) %collective-permute-start.2) | collective-permute-done | bytes 1376 | tf_op jit(solution)/shard_map/ppermute | solution.py:19
  8.9 0.1 pad_maximum_fusion.6
  9.0 1.5 %collective-permute-start.3 = (f32[7,96]{1,0:T(8,128)S(1)}, f32[7,96]{1,0:T(8,128)S(1)}, u32[]{:S(2)}, u32[]{:S(2)}) collective-permute-start(f32[7,96]{1,0:T(8,128)S(1)} %pad_maximum_fusion.6), channel_id=1, source_target_pairs={{0,4},{2,6},{4,0},{6,2},{8,12},{10,14},{12,8},{14,10},{16,20},{18,... | collective-permute-start | bytes 8072 | tf_op jit(solution)/shard_map/ppermute | solution.py:19
  10.6 2.6 %collective-permute-start.1 = (f32[5,192]{1,0:T(8,128)S(1)}, f32[5,192]{1,0:T(8,128)S(1)}, u32[]{:S(2)}, u32[]{:S(2)}) collective-permute-start(f32[5,192]{1,0:T(8,128)S(1)} %pad_maximum_fusion.4), channel_id=1, source_target_pairs={{0,16},{2,18},{4,20},{6,22},{8,24},{10,26},{12,28},{14,30},{16,0},... | collective-permute-start | bytes 11528 | tf_op jit(solution)/shard_map/ppermute | solution.py:19
  13.2 0.1 multiply_bitcast_fusion
  13.3 0.1 multiply_bitcast_fusion.1
  13.5 1.6 %collective-permute-done.1 = f32[5,192]{1,0:T(8,128)S(1)} collective-permute-done((f32[5,192]{1,0:T(8,128)S(1)}, f32[5,192]{1,0:T(8,128)S(1)}, u32[]{:S(2)}, u32[]{:S(2)}) %collective-permute-start.1) | collective-permute-done | bytes 3872 | tf_op jit(solution)/shard_map/ppermute | solution.py:19
  15.2 0.7 collective-permute-start.5
  16.0 0.1 reshape.2726
  16.0 3.6 %collective-permute-done.5 = bf16[96,3,128]{2,0,1:T(8,128)(2,1)S(1)} collective-permute-done((bf16[96,3,128]{2,0,1:T(8,128)(2,1)S(1)}, bf16[96,3,128]{2,0,1:T(8,128)(2,1)S(1)}, u32[]{:S(2)}, u32[]{:S(2)}) %collective-permute-start.5) | collective-permute-done | bytes 73760 | tf_op jit(solution)/shard_map/ppermute | solution.py:19
  19.7 3.4 %while.11 = (s32[]{:T(128)}, f32[4,96,128]{2,1,0:T(8,128)S(1)}, f32[4,5,96]{2,0,1:T(4,128)S(1)}, f32[7,192]{1,0:T(8,128)S(1)}, f32[192,1]{0,1:T(1,128)S(1)}, /*i...) while((s32[]{:T(128)}, f32[4,96,128]{2,1,0:T(8,128)S(1)}, ...), condition=%wide.region_3.4_spmd, body=%wide.region_2.3_spmd.sunk | while | flops 16626054 | bytes 485213 | solution.py:177
  19.8 0.5 fusion.98
  20.3 0.2 fusion.99
  20.6 0.5 fusion.98
  21.2 0.2 fusion.99
  21.5 0.5 fusion.98
  22.0 0.2 fusion.99
  22.3 0.5 fusion.98
  22.9 0.2 fusion.99
  23.1 2.7 %collective-permute-start.6 = (f32[192,128]{1,0:T(8,128)S(1)}, f32[192,128]{1,0:T(8,128)S(1)}, u32[]{:S(2)}, u32[]{:S(2)}) collective-permute-start(f32[192,128]{1,0:T(8,128)S(1)} %bitcast.103), channel_id=1, source_target_pairs={{0,16},{2,18},{4,20},{6,22},{8,24},{10,26},{12,28},{14,30},{16,0},... | collective-permute-start | bytes 294920 | tf_op jit(solution)/shard_map/ppermute | solution.py:19
  25.8 2.9 %collective-permute-done.6 = f32[192,128]{1,0:T(8,128)S(1)} collective-permute-done((f32[192,128]{1,0:T(8,128)S(1)}, f32[192,128]{1,0:T(8,128)S(1)}, u32[]{:S(2)}, u32[]{:S(2)}) %collective-permute-start.6) | collective-permute-done | bytes 98336 | tf_op jit(solution)/shard_map/ppermute | solution.py:19
  28.8 2.2 %collective-permute-start.7 = (f32[96,128]{1,0:T(8,128)S(1)}, f32[96,128]{1,0:T(8,128)S(1)}, u32[]{:S(2)}, u32[]{:S(2)}) collective-permute-start(f32[96,128]{1,0:T(8,128)S(1)} %slice_select_fusion.2), channel_id=1, source_target_pairs={{0,8},{2,10},{4,12},{6,14},{8,0},{10,2},{12,4},{14,6},{16,24},{18,... | collective-permute-start | bytes 147464 | tf_op jit(solution)/shard_map/ppermute | solution.py:19
  31.0 2.1 %collective-permute-done.7 = f32[96,128]{1,0:T(8,128)S(1)} collective-permute-done((f32[96,128]{1,0:T(8,128)S(1)}, f32[96,128]{1,0:T(8,128)S(1)}, u32[]{:S(2)}, u32[]{:S(2)}) %collective-permute-start.7) | collective-permute-done | bytes 49184 | tf_op jit(solution)/shard_map/ppermute | solution.py:19
  33.0 0.7 multiply_reduce_fusion
  33.8 41.7 %all-gather.1 = f32[32,1,128]{2,1,0:T(1,128)S(1)} all-gather(f32[1,1,128]{2,1,0:T(1,128)S(1)} %bitcast.108), channel_id=2, replica_groups=mesh['patch'=16,'pix'=2] {'patch','pix'}, dimensions={0}, use_global_device_ids=true | all-gather | bytes 16896 | tf_op jit(solution)/shard_map/all_gather | solution.py:12
  75.5 0.5 broadcast_multiply_fusion.2
  (50 shorter events, 0.8 us)
Async XLA Ops:
  0.6 14.6 %collective-permute-start.4 = (bf16[48,3,128]{2,0,1:T(8,128)(2,1)}, bf16[48,3,128]{2,0,1:T(8,128)(2,1)S(1)}, u32[]{:S(2)}, u32[]{:S(2)}) collective-permute-start(bf16[48,3,128]{2,0,1:T(8,128)(2,1)} %param.23), channel_id=1, source_target_pairs={{0,2},{2,0},{4,6},{6,4},{8,10},{10,8},{12,14},{14,12},{16,18},{18,... | collective-permute-start | bytes 110600 | tf_op jit(solution)/shard_map/ppermute | solution.py:19
  4.5 0.7 copy-start.3
  4.5 0.7 copy-start.6
  5.2 0.7 copy-start.1
  5.2 0.7 copy-start.2
  5.2 3.7 %collective-permute-start.2 = (f32[7,48]{1,0:T(8,128)S(1)}, f32[7,48]{1,0:T(8,128)S(1)}, u32[]{:S(2)}, u32[]{:S(2)}) collective-permute-start(f32[7,48]{1,0:T(8,128)S(1)} %stack.24), channel_id=1, source_target_pairs={{0,2},{2,0},{4,6},{6,4},{8,10},{10,8},{12,14},{14,12},{16,18},{18,... | collective-permute-start | bytes 4040 | tf_op jit(solution)/shard_map/ppermute | solution.py:19
  5.9 4.6 %collective-permute-start = (f32[5,96]{1,0:T(8,128)S(1)}, f32[5,96]{1,0:T(8,128)S(1)}, u32[]{:S(2)}, u32[]{:S(2)}) collective-permute-start(f32[5,96]{1,0:T(8,128)S(1)} %pad_maximum_fusion.5), channel_id=1, source_target_pairs={{0,8},{2,10},{4,12},{6,14},{8,0},{10,2},{12,4},{14,6},{16,24},{18,... | collective-permute-start | bytes 5768 | tf_op jit(solution)/shard_map/ppermute | solution.py:19
  9.0 4.2 %collective-permute-start.3 = (f32[7,96]{1,0:T(8,128)S(1)}, f32[7,96]{1,0:T(8,128)S(1)}, u32[]{:S(2)}, u32[]{:S(2)}) collective-permute-start(f32[7,96]{1,0:T(8,128)S(1)} %pad_maximum_fusion.6), channel_id=1, source_target_pairs={{0,4},{2,6},{4,0},{6,2},{8,12},{10,14},{12,8},{14,10},{16,20},{18,... | collective-permute-start | bytes 8072 | tf_op jit(solution)/shard_map/ppermute | solution.py:19
  10.6 4.6 %collective-permute-start.1 = (f32[5,192]{1,0:T(8,128)S(1)}, f32[5,192]{1,0:T(8,128)S(1)}, u32[]{:S(2)}, u32[]{:S(2)}) collective-permute-start(f32[5,192]{1,0:T(8,128)S(1)} %pad_maximum_fusion.4), channel_id=1, source_target_pairs={{0,16},{2,18},{4,20},{6,22},{8,24},{10,26},{12,28},{14,30},{16,0},... | collective-permute-start | bytes 11528 | tf_op jit(solution)/shard_map/ppermute | solution.py:19
  13.3 1.9 %copy-start = (bf16[48,3,128]{2,0,1:T(8,128)(2,1)S(1)}, bf16[48,3,128]{2,0,1:T(8,128)(2,1)}, u32[]{:S(2)}) copy-start(bf16[48,3,128]{2,0,1:T(8,128)(2,1)} %param.23) | copy-start | bytes 110596
  15.2 4.4 %collective-permute-start.5 = (bf16[96,3,128]{2,0,1:T(8,128)(2,1)S(1)}, bf16[96,3,128]{2,0,1:T(8,128)(2,1)S(1)}, u32[]{:S(2)}, u32[]{:S(2)}) collective-permute-start(bf16[96,3,128]{2,0,1:T(8,128)(2,1)S(1)} %pad_maximum_fusion.1), channel_id=1, source_target_pairs={{0,4},{2,6},{4,0},{6,2},{8,12},{10,14},{12,8},{14,10},{16,20},{18,... | collective-permute-start | bytes 221192 | tf_op jit(solution)/shard_map/ppermute | solution.py:19
  23.1 5.6 %collective-permute-start.6 = (f32[192,128]{1,0:T(8,128)S(1)}, f32[192,128]{1,0:T(8,128)S(1)}, u32[]{:S(2)}, u32[]{:S(2)}) collective-permute-start(f32[192,128]{1,0:T(8,128)S(1)} %bitcast.103), channel_id=1, source_target_pairs={{0,16},{2,18},{4,20},{6,22},{8,24},{10,26},{12,28},{14,30},{16,0},... | collective-permute-start | bytes 294920 | tf_op jit(solution)/shard_map/ppermute | solution.py:19
  28.7 2.2 %copy-start.7 = (s32[96]{0:T(128)S(1)}, s32[96]{0:T(128)}, u32[]{:S(2)}) copy-start(s32[96]{0:T(128)} %param.17) | copy-start | bytes 1156
  28.8 4.3 %copy-start.4 = (f32[96]{0:T(128)S(1)}, f32[96]{0:T(128)}, u32[]{:S(2)}) copy-start(f32[96]{0:T(128)} %param.16) | copy-start | bytes 1156
  28.8 4.2 %copy-start.5 = (f32[96]{0:T(128)S(1)}, f32[96]{0:T(128)}, u32[]{:S(2)}) copy-start(f32[96]{0:T(128)} %param.15) | copy-start | bytes 1156
  28.8 4.2 %collective-permute-start.7 = (f32[96,128]{1,0:T(8,128)S(1)}, f32[96,128]{1,0:T(8,128)S(1)}, u32[]{:S(2)}, u32[]{:S(2)}) collective-permute-start(f32[96,128]{1,0:T(8,128)S(1)} %slice_select_fusion.2), channel_id=1, source_target_pairs={{0,8},{2,10},{4,12},{6,14},{8,0},{10,2},{12,4},{14,6},{16,24},{18,... | collective-permute-start | bytes 147464 | tf_op jit(solution)/shard_map/ppermute | solution.py:19
